TPU v7x, 32 devices: a whole 2x2x4 slice. The times are simulated.
32 devices in a mesh: dp: 8 (over y, x, core), tensor: 4 (over z).
Axes of the slice: x: 2, y: 2, z: 4, core: 2. Of those that a mesh axis runs over, the one named last changes fastest.
Arguments:
- block_input: bfloat16 [8192, 2048], P('dp'), may hold values from -24 to 24
- segments: int32 [8192], P('dp'), may hold values from 0 to 15, never falling along the last dimension, each value on 1 to 2048 neighbouring positions
- norm_gain: bfloat16 [2048], P('dp'), may hold values from 0.5 to 1.5
- norm_bias: bfloat16 [2048], P('dp'), may hold values from -1.75 to 1.75
- qkv_weight: bfloat16 [2048, 3, 2048], P('dp', None, 'tensor'), may hold values from -1 to 1
- query_value_bias: bfloat16 [2, 32, 64], P(None, 'tensor', 'dp'), may hold values from -1.75 to 1.75
- key_bias: bfloat16 [32, 32], P('tensor', 'dp'), may hold values from -3 to 3
- dense_weight: bfloat16 [2048, 2048], P('tensor', 'dp'), may hold values from -1.5 to 1.5
- dense_bias: bfloat16 [2048], P('dp'), may hold values from -1.75 to 1.75
- up_weight: bfloat16 [2048, 8192], P('dp', 'tensor'), may hold values from -0.125 to 0.125
- up_bias: bfloat16 [128, 64], P('tensor', 'dp'), may hold values from -1.75 to 1.75
- down_weight: bfloat16 [8192, 2048], P('tensor', 'dp'), may hold values from -0.0625 to 0.0625
- down_bias: bfloat16 [2048], P('dp'), may hold values from -1.75 to 1.75
- cotangent: bfloat16 [8192, 2048], P('dp'), may hold values from -8 to 8
Outputs:
- block_output: bfloat16 [8192, 2048], P('dp')
- input_grad: float32 [8192, 2048], P('dp')
- norm_gain_grad: float32 [2048], P('dp')
- norm_bias_grad: float32 [2048], P('dp')
- qkv_weight_grad: float32 [2048, 3, 2048], P('dp', None, 'tensor')
- query_value_bias_grad: float32 [2, 32, 64], P(None, 'tensor', 'dp')
- key_bias_grad: float32 [32, 32], P('tensor', 'dp')
- dense_weight_grad: float32 [2048, 2048], P('tensor', 'dp')
- dense_bias_grad: float32 [2048], P('dp')
- up_weight_grad: float32 [2048, 8192], P('dp', 'tensor')
- up_bias_grad: float32 [128, 64], P('tensor', 'dp')
- down_weight_grad: float32 [8192, 2048], P('tensor', 'dp')
- down_bias_grad: float32 [2048], P('dp')
Inputs may be any that keep to these rules, and one draw needn't show every extreme that they name: `segments`: segment numbers never fall along the tokens; each segment has 1 to 2048 tokens, one exactly 2048.
All inputs are finite; a program needn't handle non-finite values.
Results may differ from a plain program's by a relative error of at most 0.015.
The roundings to bfloat16 on the way count: a program that leaves them out, or rounds other values in their place, can miss the bound.
Values may be sent and summed in bfloat16 or wider, within the bound.
A program may use at most 256 MiB of HBM per device.

v0:
```python
import math
import jax
import jax.numpy as jnp
from jax import lax
from jax.sharding import PartitionSpec as P

HEAD = 64
ROT = 32
SEQ = 512
EPSILON = 1e-05
SCALE = 0.125
NEGATIVE = -1e30


def rotary_tables(seg_rows):
    seq_len = seg_rows.shape[1]
    position = jnp.arange(seq_len, dtype=jnp.int32)
    starting = jnp.concatenate(
        [jnp.ones((seg_rows.shape[0], 1), dtype=jnp.bool_), seg_rows[:, 1:] != seg_rows[:, :-1]],
        axis=1,
    )
    starts = lax.cummax(jnp.where(starting, position[None, :], jnp.int32(0)), axis=1)
    offset = (position[None, :] - starts).astype(jnp.float32)
    halfway = ROT // 2
    inverse = 10000.0 ** (-(jnp.arange(halfway, dtype=jnp.float32) * (2.0 / ROT)))
    angles = offset[:, :, None] * inverse
    return (jnp.cos(angles), jnp.sin(angles))


def rotate(tensor, cosine_table, sine_table, direction):
    halfway = ROT // 2
    leading = tensor[..., :halfway]
    trailing = tensor[..., halfway:ROT]
    others = tensor[..., ROT:]
    cosine_part = cosine_table[:, :, None, :]
    sine_part = sine_table[:, :, None, :] * direction
    return jnp.concatenate(
        [
            leading * cosine_part - trailing * sine_part,
            trailing * cosine_part + leading * sine_part,
            others,
        ],
        axis=-1,
    )


def allowed_pairs(seg_rows):
    seq_len = seg_rows.shape[1]
    position = jnp.arange(seq_len, dtype=jnp.int32)
    causal = position[:, None] >= position[None, :]
    same_doc = seg_rows[:, :, None] == seg_rows[:, None, :]
    return (same_doc & causal[None])[:, None]


def gelu_tanh(inputs):
    return jax.nn.gelu(inputs, approximate=True)


def masked_scores(queries, key_rows, allowed):
    scores = (
        jnp.einsum("nqhd,nkhd->nhqk", queries, key_rows, preferred_element_type=jnp.float32) * SCALE
    )
    return jnp.where(allowed, scores, NEGATIVE)


def attend_group(placeholder, inputs):
    queries, key_rows, values, allowed = inputs
    scores = masked_scores(queries, key_rows, allowed)
    row_max = jnp.max(scores, axis=-1, keepdims=True)
    row_total = jnp.sum(jnp.exp(scores - row_max), axis=-1, keepdims=True)
    log_total = row_max + jnp.log(row_total)
    prob_low = jnp.exp(scores - log_total).astype(jnp.bfloat16)
    mixed_part = jnp.einsum(
        "nhqk,nkhd->nqhd", prob_low, values, preferred_element_type=jnp.float32
    ).astype(jnp.bfloat16)
    return (placeholder, (mixed_part, log_total))


def attend_back_group(placeholder, inputs):
    queries, key_rows, values, allowed, log_total, grad_mixed = inputs
    scores = masked_scores(queries, key_rows, allowed)
    probabilities = jnp.exp(scores - log_total)
    prob_low = probabilities.astype(jnp.bfloat16)
    grad_values = jnp.einsum(
        "nhqk,nqhd->nkhd", prob_low, grad_mixed, preferred_element_type=jnp.float32
    )
    grad_probs = jnp.einsum(
        "nqhd,nkhd->nhqk", grad_mixed, values, preferred_element_type=jnp.float32
    )
    row_delta = jnp.sum(probabilities * grad_probs, axis=-1, keepdims=True)
    grad_scores = (probabilities * (grad_probs - row_delta) * SCALE).astype(jnp.bfloat16)
    grad_queries = jnp.einsum(
        "nhqk,nkhd->nqhd", grad_scores, key_rows, preferred_element_type=jnp.float32
    )
    grad_keys = jnp.einsum(
        "nhqk,nqhd->nkhd", grad_scores, queries, preferred_element_type=jnp.float32
    )
    return (placeholder, (grad_queries, grad_keys, grad_values))


def local(
    block_input,
    segments,
    norm_gain,
    norm_bias,
    qkv_weight,
    query_value_bias,
    key_bias,
    dense_weight,
    dense_bias,
    up_weight,
    up_bias,
    down_weight,
    down_bias,
    cotangent,
):
    gathered = (
        lax.all_gather(norm_gain, "dp", axis=0, tiled=True),
        lax.all_gather(norm_bias, "dp", axis=0, tiled=True),
        lax.all_gather(qkv_weight, "dp", axis=0, tiled=True),
        lax.all_gather(query_value_bias, "dp", axis=2, tiled=True),
        lax.all_gather(key_bias, "dp", axis=1, tiled=True),
        lax.all_gather(dense_weight, "dp", axis=1, tiled=True),
        lax.all_gather(dense_bias, "dp", axis=0, tiled=True),
        lax.all_gather(up_weight, "dp", axis=0, tiled=True),
        lax.all_gather(up_bias, "dp", axis=1, tiled=True),
        lax.all_gather(down_weight, "dp", axis=1, tiled=True),
        lax.all_gather(down_bias, "dp", axis=0, tiled=True),
    )
    (
        gain_all,
        shift_all,
        qkv_all,
        qv_all,
        key_all,
        dense_all,
        dense_shift_all,
        up_all,
        up_shift_all,
        down_all,
        down_shift_all,
    ) = gathered
    row_count, model_width = block_input.shape
    local_width = qkv_all.shape[2]
    heads_here = local_width // HEAD
    seqs_here = row_count // SEQ
    per_step = math.gcd(seqs_here, max(1, 512 // SEQ))
    groups = seqs_here // per_step

    def to_groups(tensor):
        return tensor.reshape((groups, per_step) + tensor.shape[1:])

    def from_groups(tensor):
        return tensor.reshape((seqs_here,) + tensor.shape[2:])

    widened = block_input.astype(jnp.float32)
    row_mean = jnp.mean(widened, axis=1, keepdims=True)
    centred = widened - row_mean
    row_var = jnp.mean(centred * centred, axis=1, keepdims=True)
    inv_std = lax.rsqrt(row_var + EPSILON)
    normed = centred * inv_std
    normed_low = (normed * gain_all.astype(jnp.float32) + shift_all.astype(jnp.float32)).astype(
        jnp.bfloat16
    )
    qkv_flat = qkv_all.reshape(model_width, 3 * local_width)
    projected = jnp.dot(normed_low, qkv_flat, preferred_element_type=jnp.float32).reshape(
        seqs_here, SEQ, 3, heads_here, HEAD
    )
    seq_segs = segments.reshape(seqs_here, SEQ)
    cosine_table, sine_table = rotary_tables(seq_segs)
    allowed = allowed_pairs(seq_segs)
    qv_wide = qv_all.astype(jnp.float32)
    key_full = jnp.concatenate(
        [key_all.astype(jnp.float32), jnp.zeros((heads_here, HEAD - ROT), jnp.float32)], axis=1
    )
    queries = rotate(projected[:, :, 0] + qv_wide[0], cosine_table, sine_table, 1.0).astype(
        jnp.bfloat16
    )
    key_rows = rotate(projected[:, :, 1] + key_full, cosine_table, sine_table, 1.0).astype(
        jnp.bfloat16
    )
    values = (projected[:, :, 2] + qv_wide[1]).astype(jnp.bfloat16)
    placeholder = jnp.zeros((), jnp.float32)
    group_inputs = (to_groups(queries), to_groups(key_rows), to_groups(values), to_groups(allowed))
    unused, (mixed_groups, log_groups) = lax.scan(attend_group, placeholder, group_inputs)
    mixed_rows = mixed_groups.reshape(row_count, local_width)
    hidden = jnp.dot(normed_low, up_all, preferred_element_type=jnp.float32) + up_shift_all.reshape(
        -1
    ).astype(jnp.float32)
    activated = gelu_tanh(hidden).astype(jnp.bfloat16)
    branches = jnp.dot(mixed_rows, dense_all, preferred_element_type=jnp.float32) + jnp.dot(
        activated, down_all, preferred_element_type=jnp.float32
    )
    dense_shift = dense_shift_all.astype(jnp.float32)
    down_shift = down_shift_all.astype(jnp.float32)
    summed_out = lax.psum(branches, "tensor")
    block_output = (widened + summed_out + dense_shift + down_shift).astype(jnp.bfloat16)
    gain_back, qkv_back, dense_back, up_back, down_back = (
        lax.all_gather(norm_gain, "dp", axis=0, tiled=True),
        lax.all_gather(qkv_weight, "dp", axis=0, tiled=True),
        lax.all_gather(dense_weight, "dp", axis=1, tiled=True),
        lax.all_gather(up_weight, "dp", axis=0, tiled=True),
        lax.all_gather(down_weight, "dp", axis=1, tiled=True),
    )
    grad_wide = cotangent.astype(jnp.float32)
    grad_bias_out = jnp.sum(grad_wide, axis=0)
    grad_dense = jnp.dot(mixed_rows.T, cotangent, preferred_element_type=jnp.float32)
    grad_down = jnp.dot(activated.T, cotangent, preferred_element_type=jnp.float32)
    grad_mixed = (
        jnp.dot(cotangent, dense_back.T, preferred_element_type=jnp.float32)
        .astype(jnp.bfloat16)
        .reshape(seqs_here, SEQ, heads_here, HEAD)
    )
    grad_act = jnp.dot(cotangent, down_back.T, preferred_element_type=jnp.float32)
    grad_hidden = jax.vjp(gelu_tanh, hidden)[1](grad_act)[0]
    grad_up_bias = jnp.sum(grad_hidden, axis=0).reshape(up_shift_all.shape)
    grad_hidden_low = grad_hidden.astype(jnp.bfloat16)
    grad_up = jnp.dot(normed_low.T, grad_hidden_low, preferred_element_type=jnp.float32)
    back_inputs = group_inputs + (log_groups, to_groups(grad_mixed))
    unused_back, (query_groups, key_groups, value_groups) = lax.scan(
        attend_back_group, placeholder, back_inputs
    )
    grad_queries = rotate(from_groups(query_groups), cosine_table, sine_table, -1.0)
    grad_keys = rotate(from_groups(key_groups), cosine_table, sine_table, -1.0)
    grad_values = from_groups(value_groups)
    grad_qv = jnp.stack([jnp.sum(grad_queries, axis=(0, 1)), jnp.sum(grad_values, axis=(0, 1))])
    grad_key_bias = jnp.sum(grad_keys[..., :ROT], axis=(0, 1))
    grad_projected = (
        jnp.stack([grad_queries, grad_keys, grad_values], axis=2)
        .reshape(row_count, 3 * local_width)
        .astype(jnp.bfloat16)
    )
    grad_qkv = jnp.dot(normed_low.T, grad_projected, preferred_element_type=jnp.float32).reshape(
        model_width, 3, local_width
    )
    grad_normed_part = jnp.dot(
        grad_projected,
        qkv_back.reshape(model_width, 3 * local_width).T,
        preferred_element_type=jnp.float32,
    ) + jnp.dot(grad_hidden_low, up_back.T, preferred_element_type=jnp.float32)
    grad_normed = lax.psum(grad_normed_part.astype(jnp.bfloat16), "tensor").astype(jnp.float32)
    grad_gain = jnp.sum(grad_normed * normed, axis=0)
    grad_shift = jnp.sum(grad_normed, axis=0)
    scaled = grad_normed * gain_back.astype(jnp.float32)
    input_grad = (
        inv_std
        * (
            scaled
            - jnp.mean(scaled, axis=1, keepdims=True)
            - normed * jnp.mean(scaled * normed, axis=1, keepdims=True)
        )
        + grad_wide
    )
    summed = (
        lax.psum_scatter(grad_gain, "dp", scatter_dimension=0, tiled=True),
        lax.psum_scatter(grad_shift, "dp", scatter_dimension=0, tiled=True),
        lax.psum_scatter(grad_qkv, "dp", scatter_dimension=0, tiled=True),
        lax.psum_scatter(grad_qv, "dp", scatter_dimension=2, tiled=True),
        lax.psum_scatter(grad_key_bias, "dp", scatter_dimension=1, tiled=True),
        lax.psum_scatter(grad_dense, "dp", scatter_dimension=1, tiled=True),
        lax.psum_scatter(grad_bias_out, "dp", scatter_dimension=0, tiled=True),
        lax.psum_scatter(grad_up, "dp", scatter_dimension=0, tiled=True),
        lax.psum_scatter(grad_up_bias, "dp", scatter_dimension=1, tiled=True),
        lax.psum_scatter(grad_down, "dp", scatter_dimension=1, tiled=True),
    )
    return (
        block_output,
        input_grad,
        summed[0],
        summed[1],
        summed[2],
        summed[3],
        summed[4],
        summed[5],
        summed[6],
        summed[7],
        summed[8],
        summed[9],
        summed[6],
    )


def solution(mesh):
    in_specs = (
        P("dp", None),
        P("dp"),
        P("dp"),
        P("dp"),
        P("dp", None, "tensor"),
        P(None, "tensor", "dp"),
        P("tensor", "dp"),
        P("tensor", "dp"),
        P("dp"),
        P("dp", "tensor"),
        P("tensor", "dp"),
        P("tensor", "dp"),
        P("dp"),
        P("dp", None),
    )
    out_specs = (
        P("dp", None),
        P("dp", None),
        P("dp"),
        P("dp"),
        P("dp", None, "tensor"),
        P(None, "tensor", "dp"),
        P("tensor", "dp"),
        P("tensor", "dp"),
        P("dp"),
        P("dp", "tensor"),
        P("tensor", "dp"),
        P("tensor", "dp"),
        P("dp"),
    )
    return jax.shard_map(local, mesh=mesh, in_specs=in_specs, out_specs=out_specs, check_vma=False)
```

profile of v0, /device:TPU:0, one launch (start us, length us, event | category | flops | bytes accessed | tf_op | source)
XLA Modules:
  0.0 1116.1 jit_solution(14657728340286387230)
XLA Ops:
  8.0 2.3 copy.113
  15.9 2.8 convert_reduce_fusion.1
  18.7 3.5 fusion.109
  22.3 10.4 all-gather.1
  32.7 9.1 all-gather
  41.8 8.0 all-gather.2
  49.8 9.2 all_gather.45
  59.8 8.6 all_gather.41
  70.0 4.7 fusion.106
  74.7 6.2 convolution_convert_fusion
  80.9 2.8 reshape.403
  85.9 3.4 all-gather.10.cloned.1.call-done
  89.3 10.1 fusion.146
  101.6 13.5 %while.26 = (s32[]{:T(128)}, bf16[2,1,512,8,64]{2,4,3,1,0:T(8,128)(2,1)}, f32[2,1,8,512,1]{3,2,4,1,0:T(8,128)S(1)}, bf16[2,1,512,8,64]{2,4,3,1,0:T(8,128)(2,1)},...) while((s32[]{:T(128)}, ...), condition=%wide.region_7.8_spmd, body=%wide.region_4.7_spmd.sunk | while | flops 560197632 | bytes 41289912 | solution.py:185
  105.1 2.4 fusion.190
  111.7 2.4 fusion.190
  115.0 85.6 %while.27 = (s32[]{:T(128)}, f32[2,1,512,8,64]{2,4,3,1,0:T(8,128)}, f32[2,1,512,8,64]{2,4,3,1,0:T(8,128)}, f32[2,1,512,8,64]{2,4,3,1,0:T(8,128)}, bf16[2,1,512,8...) while((s32[]{:T(128)}, f32[2,1,512,8,64]{2,4,3,1,0:T(8,128)}, ...), condition=%wide.region_11.12_spmd, body=%wide.region_9.11_spmd.sunk | while | flops 1396712448 | bytes 159765776 | solution.py:220
  116.4 3.8 copy-done
  123.8 4.7 fusion.201
  128.5 14.5 %fusion.204 = f32[2,1,512,8,64]{2,4,3,1,0:T(8,128)} fusion(f32[2,1,512,8,64]{2,4,3,1,0:T(8,128)} %get-tuple-element.472, s32[]{:T(128)S(6)} %copy.169, f32[8,512,512]{1,2,0:T(8,128)} %fusion.201, f32[8,512,512]{1,2,0:T(8,128)} %copy-done, f32[8,512]{1,0:T(8,128)S(1)} %dynamic-slice_bitcast_fusion.7, ...), kind=kOutput, calls=%fused_computation.46.clone.1 | convolution fusion | flops 291508736 | bytes 35685376 | tf_op jit(solution)/shard_map/while/body/eval_jaxpr/nhqk,nqhd->nkhd/dot_general | solution.py:95
  143.0 14.4 %fusion.203 = f32[2,1,512,8,64]{2,4,3,1,0:T(8,128)} fusion(f32[2,1,512,8,64]{2,4,3,1,0:T(8,128)} %get-tuple-element.471, s32[]{:T(128)S(6)} %copy.169, f32[8,512,512]{1,2,0:T(8,128)} %fusion.201, f32[8,512,512]{1,2,0:T(8,128)} %copy-done, f32[8,512]{1,0:T(8,128)S(1)} %dynamic-slice_bitcast_fusion.7, ...), kind=kOutput, calls=%fused_computation.44.clone.1 | convolution fusion | flops 291508736 | bytes 35685376 | tf_op jit(solution)/shard_map/while/body/eval_jaxpr/nhqk,nkhd->nqhd/dot_general | solution.py:92
  158.8 3.2 copy-done
  165.7 4.7 fusion.201
  170.4 15.7 %fusion.204 = f32[2,1,512,8,64]{2,4,3,1,0:T(8,128)} fusion(f32[2,1,512,8,64]{2,4,3,1,0:T(8,128)} %get-tuple-element.472, s32[]{:T(128)S(6)} %copy.169, f32[8,512,512]{1,2,0:T(8,128)} %fusion.201, f32[8,512,512]{1,2,0:T(8,128)} %copy-done, f32[8,512]{1,0:T(8,128)S(1)} %dynamic-slice_bitcast_fusion.7, ...), kind=kOutput, calls=%fused_computation.46.clone.1 | convolution fusion | flops 291508736 | bytes 35685376 | tf_op jit(solution)/shard_map/while/body/eval_jaxpr/nhqk,nqhd->nkhd/dot_general | solution.py:95
  186.0 14.4 %fusion.203 = f32[2,1,512,8,64]{2,4,3,1,0:T(8,128)} fusion(f32[2,1,512,8,64]{2,4,3,1,0:T(8,128)} %get-tuple-element.471, s32[]{:T(128)S(6)} %copy.169, f32[8,512,512]{1,2,0:T(8,128)} %fusion.201, f32[8,512,512]{1,2,0:T(8,128)} %copy-done, f32[8,512]{1,0:T(8,128)S(1)} %dynamic-slice_bitcast_fusion.7, ...), kind=kOutput, calls=%fused_computation.44.clone.1 | convolution fusion | flops 291508736 | bytes 35685376 | tf_op jit(solution)/shard_map/while/body/eval_jaxpr/nhqk,nkhd->nqhd/dot_general | solution.py:92
  207.4 3.3 copy.129
  211.5 15.6 %fusion.147 = f32[1024,2048]{1,0:T(8,128)} fusion(bf16[1024,2048]{1,0:T(8,128)(2,1)} %fusion.106, bf16[2048,2048]{1,0:T(8,128)(2,1)} %all-gather.14.cloned.1.call-done), kind=kOutput, calls=%fused_computation.179 | convolution fusion | flops 8589934592 | bytes 20971520 | tf_op jit(solution)/shard_map/dot_general | solution.py:187
  227.1 19.2 %fusion.143 = (f32[2048]{0:T(1024)S(1)}, bf16[1024,2048]{1,0:T(8,128)(2,1)S(1)}) fusion(f32[1024,2048]{1,0:T(8,128)} %fusion.147, f32[2048]{0:T(1024)S(1)} %copy-done.25, bf16[1024,2048]{1,0:T(8,128)(2,1)} %param.31, bf16[2048,2048]{1,0:T(8,128)(2,1)} %all-gather.16.cloned.1.call-done), kind=kOutput, calls=%fused_computation.176 | convolution fusion | flops 8636069888 | bytes 25182208 | tf_op jit(solution)/shard_map/dot_general | solution.py:214
  246.4 11.1 fusion.129
  257.4 12.7 %add_convert_fusion = bf16[1024,2048]{1,0:T(8,128)(2,1)} fusion(f32[1024,2048]{1,0:T(8,128)} %fusion.129, bf16[1024,1536]{0,1:T(8,128)(2,1)S(1)} %bitcast.234, bf16[2048,1536]{0,1:T(8,128)(2,1)} %bitcast.255), kind=kOutput, calls=%fused_computation.111 | convolution fusion | flops 6446645248 | bytes 22020096 | tf_op jit(solution)/shard_map/dot_general | solution.py:236
  270.2 2.3 copy.122
  272.7 16.4 %fusion.142 = f32[1024,2048]{1,0:T(8,128)S(1)} fusion(bf16[2048,2048]{1,0:T(8,128)(2,1)} %all-gather.16.cloned.1.call-done, f32[1024,2048]{1,0:T(8,128)} %fusion.147, f32[2048]{0:T(1024)S(1)} %copy-done.25), kind=kOutput, calls=%fused_computation.175 | convolution fusion | flops 8610906112 | bytes 25174016 | tf_op jit(solution)/shard_map/dot_general | solution.py:191
  289.1 5.6 convolution_add_fusion
  295.0 6.5 fusion.148
  301.6 12.7 %fusion.121 = f32[2048,3,512]{2,0,1:T(8,128)} fusion(bf16[3,512,1024]{2,1,0:T(8,128)(2,1)} %bitcast.235, bf16[1024,2048]{1,0:T(8,128)(2,1)} %fusion.106), kind=kOutput, calls=%fused_computation.114 | convolution fusion | flops 6442450944 | bytes 19922944 | tf_op jit(solution)/shard_map/dot_general | solution.py:233
  314.3 17.3 %fusion.141 = f32[2048,2048]{1,0:T(8,128)} fusion(bf16[1024,2048]{1,0:T(8,128)(2,1)} %param.31, f32[1024,2048]{1,0:T(8,128)} %fusion.147, f32[2048]{0:T(1024)S(1)} %copy-done.25), kind=kOutput, calls=%fused_computation.174 | convolution fusion | flops 8610906112 | bytes 29368320 | tf_op jit(solution)/shard_map/dot_general | solution.py:208
  331.9 15.2 %fusion.127 = f32[2048,2048]{1,0:T(8,128)} fusion(bf16[1024,2048]{1,0:T(8,128)(2,1)} %fusion.106, bf16[1024,2048]{1,0:T(8,128)(2,1)} %copy-done.33), kind=kOutput, calls=%fused_computation.126 | convolution fusion | flops 8589934592 | bytes 25165824 | tf_op jit(solution)/shard_map/dot_general | solution.py:218
  350.3 8.6 all-gather.4
  358.9 8.3 all-gather.3
  370.3 54.7 %all-reduce.14.cloned.1.call-done = bf16[1024,2048]{1,0:T(8,128)(2,1)} async-done(((bf16[1024,2048]{1,0:T(8,128)(2,1)}), bf16[1024,2048]{1,0:T(8,128)(2,1)}) %all-reduce.14.cloned.1.call-update) | async-done | bytes 4194320 | tf_op jit(solution)/shard_map/psum | solution.py:241
  425.0 6.2 fusion.120
  431.2 285.9 %all-reduce.12.cloned.1.call-done = f32[1024,2048]{1,0:T(8,128)} async-done(((f32[1024,2048]{1,0:T(8,128)}), f32[1024,2048]{1,0:T(8,128)}) %all-reduce.12.cloned.1.call-update) | async-done | bytes 8388624 | tf_op jit(solution)/shard_map/psum | solution.py:196
  717.2 13.4 %convert_reduce_fusion.2 = (f32[2048]{0:T(1024)S(1)}, f32[1024,2048]{1,0:T(8,128)}, bf16[1024,2048]{1,0:T(8,128)(2,1)}) fusion(bf16[1024,2048]{1,0:T(8,128)(2,1)} %param.31, f32[1024]{0:T(1024)S(1)} %broadcast_multiply_fusion.1, f32[1024]{0:T(1024)S(1)} %copy-done.22, bf16[1024,2048]{1,0:T(8,128)(2,1)} %param.18, f32[1024]{0:T(1024)S(1)} %broadcast_multiply_fusion.2, ...), kind=kLoop, calls=%fused_computation.89 | loop fusion | flops 33552384 | bytes 33603584 | tf_op jit(solution)/shard_map/reduce_sum | solution.py:206
  730.6 25.7 %all-reduce.8 = (f32[2048]{0:T(1024)S(1)}, f32[2048]{0:T(1024)S(1)}, f32[2,8,64]{2,1,0:T(8,128)S(1)}, f32[8,32]{0,1:T(8,128)S(1)}, f32[2048]{0:T(1024)S(1)}, /*index=5*/f32[32,64]{1,0:T(8,128)S(1)}) all-reduce(f32[2048]{0:T(1024)S(1)} %get-tuple-element.247, ...), channel_id=2, replica_groups=mesh['dp'=8,'tensor'=4] {'dp'}, use_global_device_ids=true, to_apply=%region_16.17.clone | all-reduce | flops 9472 | bytes 75776
  759.6 12.1 %reduce-scatter.9.cloned.1.call-done = f32[512,256]{1,0:T(8,128)} async-done(((f32[512,2048]{1,0:T(8,128)}), f32[512,256]{1,0:T(8,128)}) %reduce-scatter.9.cloned.1.call-update) | async-done | bytes 524304 | tf_op jit(solution)/shard_map/reduce_scatter | solution.py:260
  771.7 96.2 %reduce-scatter.7.cloned.1.call-done = f32[256,3,512]{2,0,1:T(8,128)} async-done(((f32[2048,3,512]{2,0,1:T(8,128)}), f32[256,3,512]{2,0,1:T(8,128)}) %reduce-scatter.7.cloned.1.call-update) | async-done | bytes 1572880 | tf_op jit(solution)/shard_map/reduce_scatter | solution.py:257
  867.9 120.1 %reduce-scatter.13.cloned.1.call-done = f32[2048,256]{1,0:T(8,128)} async-done(((f32[2048,2048]{1,0:T(8,128)}), f32[2048,256]{1,0:T(8,128)}) %reduce-scatter.13.cloned.1.call-update) | async-done | bytes 2097168 | tf_op jit(solution)/shard_map/reduce_scatter | solution.py:264
  988.0 120.2 %reduce-scatter.11.cloned.1.call-done = f32[256,2048]{1,0:T(8,128)} async-done(((f32[2048,2048]{1,0:T(8,128)}), f32[256,2048]{1,0:T(8,128)}) %reduce-scatter.11.cloned.1.call-update) | async-done | bytes 2097168 | tf_op jit(solution)/shard_map/reduce_scatter | solution.py:262
  (189 shorter events, 48.3 us)
Async XLA Ops:
  7.2 34.6 %copy-start.28 = (bf16[8,4]{0,1:T(4,128)(2,1)S(1)}, bf16[8,4]{0,1:T(4,128)(2,1)}, u32[]{:S(2)}) copy-start(bf16[8,4]{0,1:T(4,128)(2,1)} %param.24) | copy-start | bytes 196
  7.2 42.6 %copy-start.27 = (bf16[32,8]{0,1:T(8,128)(2,1)S(1)}, bf16[32,8]{0,1:T(8,128)(2,1)}, u32[]{:S(2)}) copy-start(bf16[32,8]{0,1:T(8,128)(2,1)} %param.28) | copy-start | bytes 1540
  7.2 67.5 %all-gather.12.cloned.1.call-start = ((), (), s32[]{:S(2)}) async-start(), calls=%async_computation.5 | async-start | bytes 2359296 | tf_op jit(solution)/shard_map/all_gather | solution.py:123
  7.9 81.4 %all-gather.10.cloned.1.call-start = ((), (), s32[]{:S(2)}) async-start(), calls=%async_computation.4 | async-start | bytes 7077888 | tf_op jit(solution)/shard_map/all_gather | solution.py:120
  10.3 201.2 %all-gather.14.cloned.1.call-start = ((), (), s32[]{:S(2)}) async-start(), calls=%async_computation.6 | async-start | bytes 9437184 | tf_op jit(solution)/shard_map/all_gather | solution.py:125
  11.0 216.1 %all-gather.16.cloned.1.call-start = ((), (), s32[]{:S(2)}) async-start(), calls=%async_computation.7 | async-start | bytes 9437184 | tf_op jit(solution)/shard_map/all_gather | solution.py:127
  11.6 413.4 %all-reduce.14.cloned.1.call-start = ((), (), s32[]{:S(2)}) async-start(), calls=%async_computation.9 | async-start | bytes 8388608 | tf_op jit(solution)/shard_map/psum | solution.py:241
  18.7 62.2 %copy-start.21 = (f32[1024]{0:T(1024)}, f32[1024]{0:T(1024)S(1)}, u32[]{:S(2)}) copy-start(f32[1024]{0:T(1024)S(1)} %broadcast_multiply_fusion.3) | copy-start | bytes 12292
  22.2 58.6 %copy-start.23 = (f32[1024]{0:T(1024)}, f32[1024]{0:T(1024)S(1)}, u32[]{:S(2)}) copy-start(f32[1024]{0:T(1024)S(1)} %add_rsqrt_fusion) | copy-start | bytes 12292
  41.7 39.1 %copy-start.19 = (f32[8,1,256]{2,1,0:T(1,128)}, f32[8,1,256]{2,1,0:T(1,128)S(1)}, u32[]{:S(2)}) copy-start(f32[8,1,256]{2,1,0:T(1,128)S(1)} %convert_element_type.142) | copy-start | bytes 24580
  101.8 3.3 copy-start.2
  101.8 3.3 copy-start.16
  108.4 3.3 copy-start.2
  108.4 3.3 copy-start.16
  114.1 1.0 copy-start.17
  115.0 88.3 %copy-start.18 = (f32[2,512,16]{1,2,0:T(8,128)S(1)}, f32[2,512,16]{1,2,0:T(8,128)}, u32[]{:S(2)}) copy-start(f32[2,512,16]{1,2,0:T(8,128)} %get-tuple-element.316) | copy-start | bytes 196612
  115.0 5.1 copy-start.1
  115.0 5.1 copy-start.6
  115.1 8.7 copy-start.3
  116.4 3.8 copy-start
  122.4 1.4 copy-start.7
  157.4 4.6 copy-start.1
  157.4 4.6 copy-start.6
  157.5 8.2 copy-start.3
  158.8 3.2 copy-start
  164.3 1.4 copy-start.7
  200.6 6.3 copy-start.8
  203.4 2.5 copy-start.4
  205.6 1.2 copy-start.12
  205.6 1.3 copy-start.13
  211.5 45.9 %copy-start.14 = (bf16[192,8,2,512]{3,1,2,0:T(8,128)(2,1)}, bf16[192,8,2,512]{3,1,2,0:T(8,128)(2,1)S(1)}, u32[]{:S(2)}) copy-start(bf16[192,8,2,512]{3,1,2,0:T(8,128)(2,1)S(1)} %copy.149) | copy-start | bytes 9437188
  211.5 15.6 %copy-start.25 = (f32[2048]{0:T(1024)S(1)}, f32[2048]{0:T(1024)}, u32[]{:S(2)}) copy-start(f32[2048]{0:T(1024)} %reshape.385) | copy-start | bytes 24580
  227.1 19.2 %copy-start.29 = (bf16[2048,2048]{1,0:T(8,128)(2,1)S(1)}, bf16[2048,2048]{1,0:T(8,128)(2,1)}, u32[]{:S(2)}) copy-start(bf16[2048,2048]{1,0:T(8,128)(2,1)} %all-gather.14.cloned.1.call-done) | copy-start | bytes 25165828
  246.3 11.1 copy-start.33
  270.1 447.1 %all-reduce.12.cloned.1.call-start = ((), (), s32[]{:S(2)}) async-start(), calls=%async_computation.8 | async-start | bytes 16777216 | tf_op jit(solution)/shard_map/psum | solution.py:196
  272.7 16.4 %copy-start.15 = (bf16[512,2048]{1,0:T(8,128)(2,1)S(1)}, bf16[512,2048]{1,0:T(8,128)(2,1)}, u32[]{:S(2)}) copy-start(bf16[512,2048]{1,0:T(8,128)(2,1)} %all-gather.12.cloned.1.call-done) | copy-start | bytes 6291460
  294.8 476.9 %reduce-scatter.9.cloned.1.call-start = ((), (), s32[]{:S(2)}) async-start(), calls=%async_computation.11 | async-start | bytes 4718592 | tf_op jit(solution)/shard_map/reduce_scatter | solution.py:260
  301.5 566.4 %reduce-scatter.7.cloned.1.call-start = ((), (), s32[]{:S(2)}) async-start(), calls=%async_computation.10 | async-start | bytes 14155776 | tf_op jit(solution)/shard_map/reduce_scatter | solution.py:257
  314.2 673.8 %reduce-scatter.13.cloned.1.call-start = ((), (), s32[]{:S(2)}) async-start(), calls=%async_computation.13 | async-start | bytes 18874368 | tf_op jit(solution)/shard_map/reduce_scatter | solution.py:264
  331.6 776.7 %reduce-scatter.11.cloned.1.call-start = ((), (), s32[]{:S(2)}) async-start(), calls=%async_computation.12 | async-start | bytes 18874368 | tf_op jit(solution)/shard_map/reduce_scatter | solution.py:262
  347.1 3.2 copy-start.30
  347.1 3.2 copy-start.31
  347.1 20.1 %copy-start.9 = (f32[2,1,512,8,64]{2,4,3,1,0:T(8,128)S(1)}, f32[2,1,512,8,64]{2,4,3,1,0:T(8,128)}, u32[]{:S(2)}) copy-start(f32[2,1,512,8,64]{2,4,3,1,0:T(8,128)} %get-tuple-element.109) | copy-start | bytes 6291460
  347.1 21.7 %copy-start.5 = (f32[2,512,8,32]{1,3,2,0:T(8,128)S(1)}, f32[2,512,8,32]{1,3,2,0:T(8,128)}, u32[]{:S(2)}) copy-start(f32[2,512,8,32]{1,3,2,0:T(8,128)} %copy-done.4) | copy-start | bytes 3145732
  347.1 77.9 %copy-start.20 = (f32[8,1,256]{2,1,0:T(1,128)S(1)}, f32[8,1,256]{2,1,0:T(1,128)}, u32[]{:S(2)}) copy-start(f32[8,1,256]{2,1,0:T(1,128)} %copy-done.19) | copy-start | bytes 24580
  347.1 77.9 %copy-start.22 = (f32[1024]{0:T(1024)S(1)}, f32[1024]{0:T(1024)}, u32[]{:S(2)}) copy-start(f32[1024]{0:T(1024)} %copy-done.21) | copy-start | bytes 12292
  347.1 77.9 %copy-start.24 = (f32[1024]{0:T(1024)S(1)}, f32[1024]{0:T(1024)}, u32[]{:S(2)}) copy-start(f32[1024]{0:T(1024)} %copy-done.23) | copy-start | bytes 12292
  757.0 351.8 %copy-start.26 = (f32[256]{0:T(256)}, f32[256]{0:T(256)S(1)}, u32[]{:S(2)}) copy-start(f32[256]{0:T(256)S(1)} %dynamic-slice.9) | copy-start | bytes 3076
  (4 other events, 3.4 us)
Sparse Core Ops, SparseCore 0:
  9.9 30.8 all-gather.11
  42.6 46.6 all-gather.9
  91.2 54.2 all-gather.13
  147.2 55.8 all-gather.15
  270.2 154.7 all-reduce.13
  427.3 289.7 all-reduce.11
  721.1 50.5 reduce-scatter.8
  775.7 92.0 reduce-scatter.6
  872.0 115.9 reduce-scatter.12
  992.0 116.2 reduce-scatter.10
where the time goes:
time: 1120 us
  waiting for transfers between devices  695 us (62%)
  matrix products  232 us (21%)
  blocking collectives  87.8 us (8%)
  other arithmetic  44.5 us (4%)
  local copies, waits for them, and re-layouts  39 us (3%)
  between operations  17.1 us (2%)
    psum x1, waiting for transfers between devices, local(): summed_out = lax.psum(branches, 'tensor')  286 us
    reduce_scatter x1, waiting for transfers between devices, local(): lax.psum_scatter(grad_up, 'dp', scatter_dimension=0, tiled=True)  120 us
    reduce_scatter x1, waiting for transfers between devices, local(): lax.psum_scatter(grad_down, 'dp', scatter_dimension=1, tiled=True)  120 us
    reduce_scatter x1, waiting for transfers between devices, local(): lax.psum_scatter(grad_qkv, 'dp', scatter_dimension=0, tiled=True)  96.2 us
    psum x1, waiting for transfers between devices, local(): lax.psum(grad_normed_part.astype(jnp.bfloat16), 'tensor')  54.7 us
    dot_general x2, matrix products, attend_back_group(): jnp.einsum('nhqk,nqhd->nkhd', grad_scores, queries, preferred_element_typ...  30.2 us
    dot_general x2, matrix products, attend_back_group(): jnp.einsum('nhqk,nkhd->nqhd', grad_scores, key_rows, preferred_element_ty...  28.8 us
    unnamed x1, blocking collectives  25.7 us
  transfers between devices with their start and end apart: 10, of which 7 were waited for; matrix products, arithmetic and copies ran while one was open for 23% of the time, Pallas kernels for 0%

commit v1 on v0

--- a/solution.py
+++ b/solution.py
@@ -10,6 +10,14 @@
 EPSILON = 1e-05
 SCALE = 0.125
 NEGATIVE = -1e30
+
+
+def added_up(block, name):
+    size, acc = (lax.axis_size(name), block)
+    for reach in [1 << k for k in range(size.bit_length() - 1)]:
+        swap = [(i, i ^ reach) for i in range(size)]
+        acc = acc + lax.ppermute(acc, name, swap)
+    return acc
 
 
 def rotary_tables(seg_rows):
@@ -193,7 +201,7 @@
     )
     dense_shift = dense_shift_all.astype(jnp.float32)
     down_shift = down_shift_all.astype(jnp.float32)
-    summed_out = lax.psum(branches, "tensor")
+    summed_out = added_up(branches, "tensor")
     block_output = (widened + summed_out + dense_shift + down_shift).astype(jnp.bfloat16)
     gain_back, qkv_back, dense_back, up_back, down_back = (
         lax.all_gather(norm_gain, "dp", axis=0, tiled=True),

time: 1120 us -> 1020 us (0.911)
  waiting for transfers between devices: 695 us -> 586 us
  other arithmetic: 44.5 us -> 59.1 us
    ppermute x0 -> x2, waiting for transfers between devices: none -> 580 us  [added_up(): acc = acc + lax.ppermute(acc, name, swap)]
    psum x1 -> x0, waiting for transfers between devices: 286 us -> none  [local(): summed_out = lax.psum(branches, 'tensor')]
    reduce_scatter x1, waiting for transfers between devices: 120 us -> 0.01 us  [local(): lax.psum_scatter(grad_up, 'dp', scatter_dimension=0, tiled=True)]
    reduce_scatter x1, waiting for transfers between devices: 120 us -> 0.01 us  [local(): lax.psum_scatter(grad_down, 'dp', scatter_dimension=1, tiled=True)]
    reduce_scatter x1, waiting for transfers between devices: 96.2 us -> 0.01 us  [local(): lax.psum_scatter(grad_qkv, 'dp', scatter_dimension=0, tiled=True)]
    psum x1, waiting for transfers between devices: 54.7 us -> 0.01 us  [local(): lax.psum(grad_normed_part.astype(jnp.bfloat16), 'tensor')]
    add x0 -> x1, other arithmetic: none -> 12.3 us  [added_up(): acc = acc + lax.ppermute(acc, name, swap)]
    reduce_scatter x1, waiting for transfers between devices: 12.1 us -> 0.01 us  [local(): lax.psum_scatter(grad_dense, 'dp', scatter_dimension=1, tiled=True)]
  transfers between devices with their start and end apart: 10 -> 11, of which waited for: 7 -> 3; matrix products, arithmetic and copies ran while one was open for 23% -> 26% of each run, Pallas kernels for 0% -> 0%
where the time goes in v1:
time: 1020 us
  waiting for transfers between devices  586 us (57%)
  matrix products  228 us (22%)
  blocking collectives  84.9 us (8%)
  other arithmetic  59.1 us (6%)
  local copies, waits for them, and re-layouts  41.8 us (4%)
  between operations  16.6 us (2%)
    ppermute x2, waiting for transfers between devices, added_up(): acc = acc + lax.ppermute(acc, name, swap)  580 us
    dot_general x2, matrix products, attend_back_group(): jnp.einsum('nhqk,nqhd->nkhd', grad_scores, queries, preferred_element_typ...  30.2 us
    dot_general x2, matrix products, attend_back_group(): jnp.einsum('nhqk,nkhd->nqhd', grad_scores, key_rows, preferred_element_ty...  28.8 us
    unnamed x1, blocking collectives  22.9 us
  transfers between devices with their start and end apart: 11, of which 3 were waited for; matrix products, arithmetic and copies ran while one was open for 26% of the time, Pallas kernels for 0%

profile of v1, /device:TPU:0, one launch (start us, length us, event | category | flops | bytes accessed | tf_op | source)
XLA Modules:
  0.0 1020.9 jit_solution(14425690304880803611)
XLA Ops:
  8.0 2.4 copy.113
  15.9 2.8 convert_reduce_fusion.1
  18.8 3.5 fusion.109
  22.3 10.4 %all-gather.1 = bf16[8,1,256]{2,1,0:T(2,128)(2,1)S(1)} all-gather(bf16[1,1,256]{2,1,0:T(2,128)(2,1)S(1)} %reshape.388), channel_id=1, replica_groups=mesh['dp'=8,'tensor'=4] {'dp'}, dimensions={0}, use_global_device_ids=true | all-gather | bytes 4608 | tf_op jit(solution)/shard_map/all_gather | solution.py:127
  32.8 9.1 all-gather
  41.8 8.0 all-gather.2
  49.9 9.2 all_gather.45
  59.9 8.3 all_gather.41
  69.7 4.7 fusion.106
  74.4 6.2 convolution_convert_fusion
  80.6 2.8 reshape.403
  85.7 3.6 all-gather.10.cloned.1.call-done
  89.3 10.1 fusion.146
  101.5 13.5 %while.26 = (s32[]{:T(128)}, bf16[2,1,512,8,64]{2,4,3,1,0:T(8,128)(2,1)}, f32[2,1,8,512,1]{3,2,4,1,0:T(8,128)S(1)}, bf16[2,1,512,8,64]{2,4,3,1,0:T(8,128)(2,1)},...) while((s32[]{:T(128)}, ...), condition=%wide.region_7.8_spmd, body=%wide.region_4.7_spmd.sunk | while | flops 560197632 | bytes 41289912 | solution.py:193
  105.0 2.4 fusion.190
  111.7 2.4 fusion.190
  115.0 85.7 %while.27 = (s32[]{:T(128)}, f32[2,1,512,8,64]{2,4,3,1,0:T(8,128)}, f32[2,1,512,8,64]{2,4,3,1,0:T(8,128)}, f32[2,1,512,8,64]{2,4,3,1,0:T(8,128)}, bf16[2,1,512,8...) while((s32[]{:T(128)}, f32[2,1,512,8,64]{2,4,3,1,0:T(8,128)}, ...), condition=%wide.region_10.11_spmd, body=%wide.region_8.10_spmd.sunk | while | flops 1396712448 | bytes 159765776 | solution.py:228
  116.4 3.8 copy-done
  120.2 2.3 fusion.205
  123.8 4.7 fusion.201
  128.5 14.5 %fusion.204 = f32[2,1,512,8,64]{2,4,3,1,0:T(8,128)} fusion(f32[2,1,512,8,64]{2,4,3,1,0:T(8,128)} %get-tuple-element.472, s32[]{:T(128)S(6)} %copy.169, f32[8,512,512]{1,2,0:T(8,128)} %fusion.201, f32[8,512,512]{1,2,0:T(8,128)} %copy-done, f32[8,512]{1,0:T(8,128)S(1)} %dynamic-slice_bitcast_fusion.7, ...), kind=kOutput, calls=%fused_computation.46.clone.1 | convolution fusion | flops 291508736 | bytes 35685376 | tf_op jit(solution)/shard_map/while/body/eval_jaxpr/nhqk,nqhd->nkhd/dot_general | solution.py:103
  143.0 14.4 %fusion.203 = f32[2,1,512,8,64]{2,4,3,1,0:T(8,128)} fusion(f32[2,1,512,8,64]{2,4,3,1,0:T(8,128)} %get-tuple-element.471, s32[]{:T(128)S(6)} %copy.169, f32[8,512,512]{1,2,0:T(8,128)} %fusion.201, f32[8,512,512]{1,2,0:T(8,128)} %copy-done, f32[8,512]{1,0:T(8,128)S(1)} %dynamic-slice_bitcast_fusion.7, ...), kind=kOutput, calls=%fused_computation.44.clone.1 | convolution fusion | flops 291508736 | bytes 35685376 | tf_op jit(solution)/shard_map/while/body/eval_jaxpr/nhqk,nkhd->nqhd/dot_general | solution.py:100
  158.8 3.2 copy-done
  162.0 2.3 fusion.205
  165.6 4.7 fusion.201
  170.3 15.7 %fusion.204 = f32[2,1,512,8,64]{2,4,3,1,0:T(8,128)} fusion(f32[2,1,512,8,64]{2,4,3,1,0:T(8,128)} %get-tuple-element.472, s32[]{:T(128)S(6)} %copy.169, f32[8,512,512]{1,2,0:T(8,128)} %fusion.201, f32[8,512,512]{1,2,0:T(8,128)} %copy-done, f32[8,512]{1,0:T(8,128)S(1)} %dynamic-slice_bitcast_fusion.7, ...), kind=kOutput, calls=%fused_computation.46.clone.1 | convolution fusion | flops 291508736 | bytes 35685376 | tf_op jit(solution)/shard_map/while/body/eval_jaxpr/nhqk,nqhd->nkhd/dot_general | solution.py:103
  186.0 14.4 %fusion.203 = f32[2,1,512,8,64]{2,4,3,1,0:T(8,128)} fusion(f32[2,1,512,8,64]{2,4,3,1,0:T(8,128)} %get-tuple-element.471, s32[]{:T(128)S(6)} %copy.169, f32[8,512,512]{1,2,0:T(8,128)} %fusion.201, f32[8,512,512]{1,2,0:T(8,128)} %copy-done, f32[8,512]{1,0:T(8,128)S(1)} %dynamic-slice_bitcast_fusion.7, ...), kind=kOutput, calls=%fused_computation.44.clone.1 | convolution fusion | flops 291508736 | bytes 35685376 | tf_op jit(solution)/shard_map/while/body/eval_jaxpr/nhqk,nkhd->nqhd/dot_general | solution.py:100
  207.5 3.3 copy.129
  211.7 15.6 %fusion.147 = f32[1024,2048]{1,0:T(8,128)} fusion(bf16[1024,2048]{1,0:T(8,128)(2,1)} %fusion.106, bf16[2048,2048]{1,0:T(8,128)(2,1)} %all-gather.14.cloned.1.call-done), kind=kOutput, calls=%fused_computation.179 | convolution fusion | flops 8589934592 | bytes 20971520 | tf_op jit(solution)/shard_map/dot_general | solution.py:195
  227.2 18.9 %fusion.143 = (f32[2048]{0:T(1024)S(1)}, bf16[1024,2048]{1,0:T(8,128)(2,1)S(1)}) fusion(f32[1024,2048]{1,0:T(8,128)} %fusion.147, f32[2048]{0:T(1024)S(1)} %copy-done.28, bf16[1024,2048]{1,0:T(8,128)(2,1)} %param.31, bf16[2048,2048]{1,0:T(8,128)(2,1)} %all-gather.16.cloned.1.call-done), kind=kOutput, calls=%fused_computation.176 | convolution fusion | flops 8636069888 | bytes 25182208 | tf_op jit(solution)/shard_map/dot_general | solution.py:222
  246.2 11.2 %fusion.129 = f32[1024,2048]{1,0:T(8,128)} fusion(bf16[2048,2048]{1,0:T(8,128)(2,1)S(1)} %copy-done.32, bf16[1024,2048]{1,0:T(8,128)(2,1)S(1)} %get-tuple-element.294), kind=kOutput, calls=%fused_computation.128 | convolution fusion | flops 8589934592 | bytes 20971520 | tf_op jit(solution)/shard_map/dot_general | solution.py:248
  257.4 12.7 %add_convert_fusion = bf16[1024,2048]{1,0:T(8,128)(2,1)} fusion(f32[1024,2048]{1,0:T(8,128)} %fusion.129, bf16[1024,1536]{0,1:T(8,128)(2,1)S(1)} %bitcast.234, bf16[2048,1536]{0,1:T(8,128)(2,1)} %bitcast.255), kind=kOutput, calls=%fused_computation.111 | convolution fusion | flops 6446645248 | bytes 22020096 | tf_op jit(solution)/shard_map/dot_general | solution.py:244
  270.1 2.3 copy.122
  272.7 6.5 fusion.148
  279.3 12.6 %fusion.121 = f32[2048,3,512]{2,0,1:T(8,128)} fusion(bf16[3,512,1024]{2,1,0:T(8,128)(2,1)} %bitcast.235, bf16[1024,2048]{1,0:T(8,128)(2,1)} %fusion.106), kind=kOutput, calls=%fused_computation.114 | convolution fusion | flops 6442450944 | bytes 19922944 | tf_op jit(solution)/shard_map/dot_general | solution.py:241
  292.0 17.6 %fusion.141 = f32[2048,2048]{1,0:T(8,128)} fusion(bf16[1024,2048]{1,0:T(8,128)(2,1)} %param.31, f32[1024,2048]{1,0:T(8,128)} %fusion.147, f32[2048]{0:T(1024)S(1)} %copy-done.28), kind=kOutput, calls=%fused_computation.174 | convolution fusion | flops 8610906112 | bytes 29368320 | tf_op jit(solution)/shard_map/dot_general | solution.py:216
  309.6 15.3 %fusion.127 = f32[2048,2048]{1,0:T(8,128)} fusion(bf16[1024,2048]{1,0:T(8,128)(2,1)} %fusion.106, bf16[1024,2048]{1,0:T(8,128)(2,1)} %copy-done.36), kind=kOutput, calls=%fused_computation.126 | convolution fusion | flops 8589934592 | bytes 25165824 | tf_op jit(solution)/shard_map/dot_general | solution.py:226
  325.0 15.8 %fusion.142 = f32[1024,2048]{1,0:T(8,128)S(1)} fusion(bf16[2048,2048]{1,0:T(8,128)(2,1)} %all-gather.16.cloned.1.call-done, f32[1024,2048]{1,0:T(8,128)} %fusion.147, f32[2048]{0:T(1024)S(1)} %copy-done.28), kind=kOutput, calls=%fused_computation.175 | convolution fusion | flops 8610906112 | bytes 25174016 | tf_op jit(solution)/shard_map/dot_general | solution.py:199
  340.8 2.5 convolution_add_fusion
  343.3 3.4 copy-done.2
  348.1 248.8 %collective-permute-done = f32[1024,2048]{1,0:T(8,128)} collective-permute-done((f32[1024,2048]{1,0:T(8,128)S(1)}, f32[1024,2048]{1,0:T(8,128)}, u32[]{:S(2)}, u32[]{:S(2)}) %collective-permute-start) | collective-permute-done | bytes 8388640 | tf_op jit(solution)/shard_map/ppermute | solution.py:19
  596.9 12.3 %add.184 = f32[1024,2048]{1,0:T(8,128)} add(f32[1024,2048]{1,0:T(8,128)} %copy-done.2, f32[1024,2048]{1,0:T(8,128)} %collective-permute-done) | non-fusion elementwise | flops 2097152 | bytes 25165824 | tf_op jit(solution)/shard_map/add | solution.py:19
  614.0 8.9 all-gather.4
  622.9 8.3 all-gather.3
  634.4 6.4 fusion.120
  640.8 331.2 %collective-permute-done.1 = f32[1024,2048]{1,0:T(8,128)} collective-permute-done((f32[1024,2048]{1,0:T(8,128)}, f32[1024,2048]{1,0:T(8,128)}, u32[]{:S(2)}, u32[]{:S(2)}) %collective-permute-start.1) | collective-permute-done | bytes 8388640 | tf_op jit(solution)/shard_map/ppermute | solution.py:19
  971.9 15.5 %convert_reduce_fusion.2 = (f32[2048]{0:T(1024)S(1)}, f32[1024,2048]{1,0:T(8,128)}, bf16[1024,2048]{1,0:T(8,128)(2,1)}) fusion(bf16[1024,2048]{1,0:T(8,128)(2,1)} %param.31, f32[1024]{0:T(1024)S(1)} %broadcast_multiply_fusion.1, f32[1024]{0:T(1024)S(1)} %copy-done.25, bf16[1024,2048]{1,0:T(8,128)(2,1)S(1)} %copy-done.1, ...), kind=kLoop, calls=%fused_computation.89 | loop fusion | flops 35649536 | bytes 41992192 | tf_op jit(solution)/shard_map/reduce_sum | solution.py:214
  987.4 22.9 %all-reduce.8 = (f32[2048]{0:T(1024)S(1)}, f32[2048]{0:T(1024)S(1)}, f32[2,8,64]{2,1,0:T(8,128)S(1)}, f32[8,32]{0,1:T(8,128)S(1)}, f32[2048]{0:T(1024)S(1)}, /*index=5*/f32[32,64]{1,0:T(8,128)S(1)}) all-reduce(f32[2048]{0:T(1024)S(1)} %get-tuple-element.247, ...), channel_id=2, replica_groups=mesh['dp'=8,'tensor'=4] {'dp'}, use_global_device_ids=true, to_apply=%region_15.16.clone | all-reduce | flops 9472 | bytes 75776
  (197 shorter events, 46.3 us)
Async XLA Ops:
  7.2 34.7 %copy-start.31 = (bf16[8,4]{0,1:T(4,128)(2,1)S(1)}, bf16[8,4]{0,1:T(4,128)(2,1)}, u32[]{:S(2)}) copy-start(bf16[8,4]{0,1:T(4,128)(2,1)} %param.24) | copy-start | bytes 196
  7.2 42.7 %copy-start.30 = (bf16[32,8]{0,1:T(8,128)(2,1)S(1)}, bf16[32,8]{0,1:T(8,128)(2,1)}, u32[]{:S(2)}) copy-start(bf16[32,8]{0,1:T(8,128)(2,1)} %param.28) | copy-start | bytes 1540
  7.2 67.2 %all-gather.12.cloned.1.call-start = ((), (), s32[]{:S(2)}) async-start(), calls=%async_computation.5 | async-start | bytes 2359296 | tf_op jit(solution)/shard_map/all_gather | solution.py:131
  7.9 81.4 %all-gather.10.cloned.1.call-start = ((), (), s32[]{:S(2)}) async-start(), calls=%async_computation.4 | async-start | bytes 7077888 | tf_op jit(solution)/shard_map/all_gather | solution.py:128
  10.4 201.3 %all-gather.14.cloned.1.call-start = ((), (), s32[]{:S(2)}) async-start(), calls=%async_computation.6 | async-start | bytes 9437184 | tf_op jit(solution)/shard_map/all_gather | solution.py:133
  11.1 216.1 %all-gather.16.cloned.1.call-start = ((), (), s32[]{:S(2)}) async-start(), calls=%async_computation.7 | async-start | bytes 9437184 | tf_op jit(solution)/shard_map/all_gather | solution.py:135
  11.7 622.7 %all-reduce.11.cloned.1.call-start = ((), (), s32[]{:S(2)}) async-start(), calls=%async_computation.8 | async-start | bytes 8388608 | tf_op jit(solution)/shard_map/psum | solution.py:249
  18.8 61.9 %copy-start.24 = (f32[1024]{0:T(1024)}, f32[1024]{0:T(1024)S(1)}, u32[]{:S(2)}) copy-start(f32[1024]{0:T(1024)S(1)} %broadcast_multiply_fusion.3) | copy-start | bytes 12292
  22.3 58.3 %copy-start.26 = (f32[1024]{0:T(1024)}, f32[1024]{0:T(1024)S(1)}, u32[]{:S(2)}) copy-start(f32[1024]{0:T(1024)S(1)} %add_rsqrt_fusion) | copy-start | bytes 12292
  41.8 38.8 %copy-start.22 = (f32[8,1,256]{2,1,0:T(1,128)}, f32[8,1,256]{2,1,0:T(1,128)S(1)}, u32[]{:S(2)}) copy-start(f32[8,1,256]{2,1,0:T(1,128)S(1)} %convert_element_type.142) | copy-start | bytes 24580
  101.8 3.3 copy-start.5
  101.8 3.3 copy-start.19
  108.4 3.3 copy-start.5
  108.4 3.3 copy-start.19
  115.0 88.5 %copy-start.21 = (f32[2,512,16]{1,2,0:T(8,128)S(1)}, f32[2,512,16]{1,2,0:T(8,128)}, u32[]{:S(2)}) copy-start(f32[2,512,16]{1,2,0:T(8,128)} %get-tuple-element.316) | copy-start | bytes 196612
  115.0 5.1 copy-start.4
  115.0 5.1 copy-start.9
  115.1 8.7 copy-start.6
  116.4 3.8 copy-start
  157.4 4.6 copy-start.4
  157.4 4.6 copy-start.9
  157.5 8.2 copy-start.6
  158.8 3.2 copy-start
  200.8 6.3 copy-start.11
  203.5 2.5 copy-start.7
  211.6 45.8 %copy-start.17 = (bf16[192,8,2,512]{3,1,2,0:T(8,128)(2,1)}, bf16[192,8,2,512]{3,1,2,0:T(8,128)(2,1)S(1)}, u32[]{:S(2)}) copy-start(bf16[192,8,2,512]{3,1,2,0:T(8,128)(2,1)S(1)} %copy.149) | copy-start | bytes 9437188
  211.6 15.6 %copy-start.28 = (f32[2048]{0:T(1024)S(1)}, f32[2048]{0:T(1024)}, u32[]{:S(2)}) copy-start(f32[2048]{0:T(1024)} %reshape.385) | copy-start | bytes 24580
  227.2 19.0 %copy-start.32 = (bf16[2048,2048]{1,0:T(8,128)(2,1)S(1)}, bf16[2048,2048]{1,0:T(8,128)(2,1)}, u32[]{:S(2)}) copy-start(bf16[2048,2048]{1,0:T(8,128)(2,1)} %all-gather.14.cloned.1.call-done) | copy-start | bytes 25165828
  246.2 11.2 %copy-start.36 = (bf16[1024,2048]{1,0:T(8,128)(2,1)}, bf16[1024,2048]{1,0:T(8,128)(2,1)S(1)}, u32[]{:S(2)}) copy-start(bf16[1024,2048]{1,0:T(8,128)(2,1)S(1)} %get-tuple-element.294) | copy-start | bytes 12582916
  270.1 743.5 %reduce-scatter.9.cloned.1.call-start = ((), (), s32[]{:S(2)}) async-start(), calls=%async_computation.10 | async-start | bytes 4718592 | tf_op jit(solution)/shard_map/reduce_scatter | solution.py:268
  279.2 734.4 %reduce-scatter.7.cloned.1.call-start = ((), (), s32[]{:S(2)}) async-start(), calls=%async_computation.9 | async-start | bytes 14155776 | tf_op jit(solution)/shard_map/reduce_scatter | solution.py:265
  291.9 721.7 %reduce-scatter.13.cloned.1.call-start = ((), (), s32[]{:S(2)}) async-start(), calls=%async_computation.12 | async-start | bytes 18874368 | tf_op jit(solution)/shard_map/reduce_scatter | solution.py:272
  309.6 704.0 %reduce-scatter.11.cloned.1.call-start = ((), (), s32[]{:S(2)}) async-start(), calls=%async_computation.11 | async-start | bytes 18874368 | tf_op jit(solution)/shard_map/reduce_scatter | solution.py:270
  325.0 15.8 %copy-start.18 = (bf16[512,2048]{1,0:T(8,128)(2,1)S(1)}, bf16[512,2048]{1,0:T(8,128)(2,1)}, u32[]{:S(2)}) copy-start(bf16[512,2048]{1,0:T(8,128)(2,1)} %all-gather.12.cloned.1.call-done) | copy-start | bytes 6291460
  343.3 3.4 copy-start.2
  346.7 264.8 %copy-start.35 = (u32[32]{0:T(128)S(1)}, u32[32]{0:T(128)}, u32[]{:S(2)}) copy-start(u32[32]{0:T(128)} %constant.93) | copy-start | bytes 388
  346.7 267.3 %copy-start.33 = (bf16[256]{0:T(256)(128)(2,1)S(1)}, bf16[256]{0:T(256)(128)(2,1)}, u32[]{:S(2)}) copy-start(bf16[256]{0:T(256)(128)(2,1)} %param.26) | copy-start | bytes 1540
  346.7 267.3 %copy-start.34 = (bf16[256]{0:T(256)(128)(2,1)S(1)}, bf16[256]{0:T(256)(128)(2,1)}, u32[]{:S(2)}) copy-start(bf16[256]{0:T(256)(128)(2,1)} %param.30) | copy-start | bytes 1540
  346.7 284.5 %copy-start.12 = (f32[2,1,512,8,64]{2,4,3,1,0:T(8,128)S(1)}, f32[2,1,512,8,64]{2,4,3,1,0:T(8,128)}, u32[]{:S(2)}) copy-start(f32[2,1,512,8,64]{2,4,3,1,0:T(8,128)} %get-tuple-element.109) | copy-start | bytes 6291460
  346.7 286.1 %copy-start.8 = (f32[2,512,8,32]{1,3,2,0:T(8,128)S(1)}, f32[2,512,8,32]{1,3,2,0:T(8,128)}, u32[]{:S(2)}) copy-start(f32[2,512,8,32]{1,3,2,0:T(8,128)} %copy-done.7) | copy-start | bytes 3145732
  346.7 287.7 %copy-start.23 = (f32[8,1,256]{2,1,0:T(1,128)S(1)}, f32[8,1,256]{2,1,0:T(1,128)}, u32[]{:S(2)}) copy-start(f32[8,1,256]{2,1,0:T(1,128)} %copy-done.22) | copy-start | bytes 24580
  346.7 287.7 %copy-start.25 = (f32[1024]{0:T(1024)S(1)}, f32[1024]{0:T(1024)}, u32[]{:S(2)}) copy-start(f32[1024]{0:T(1024)} %copy-done.24) | copy-start | bytes 12292
  346.7 287.6 %copy-start.27 = (f32[1024]{0:T(1024)S(1)}, f32[1024]{0:T(1024)}, u32[]{:S(2)}) copy-start(f32[1024]{0:T(1024)} %copy-done.26) | copy-start | bytes 12292
  346.7 250.2 %collective-permute-start = (f32[1024,2048]{1,0:T(8,128)S(1)}, f32[1024,2048]{1,0:T(8,128)}, u32[]{:S(2)}, u32[]{:S(2)}) collective-permute-start(f32[1024,2048]{1,0:T(8,128)S(1)} %convolution_add_fusion), channel_id=1, source_target_pairs={{0,1},{1,0},{2,3},{3,2},{4,5},{5,4},{6,7},{7,6},{8,9},{9,8},{10,11... | collective-permute-start | bytes 25165832 | tf_op jit(solution)/shard_map/ppermute | solution.py:19
  609.2 362.7 %collective-permute-start.1 = (f32[1024,2048]{1,0:T(8,128)}, f32[1024,2048]{1,0:T(8,128)}, u32[]{:S(2)}, u32[]{:S(2)}) collective-permute-start(f32[1024,2048]{1,0:T(8,128)} %add.184), channel_id=1, source_target_pairs={{0,2},{1,3},{2,0},{3,1},{4,6},{5,7},{6,4},{7,5},{8,10},{9,11},{10,... | collective-permute-start | bytes 25165832 | tf_op jit(solution)/shard_map/ppermute | solution.py:19
  634.4 337.6 %copy-start.1 = (bf16[1024,2048]{1,0:T(8,128)(2,1)S(1)}, bf16[1024,2048]{1,0:T(8,128)(2,1)}, u32[]{:S(2)}) copy-start(bf16[1024,2048]{1,0:T(8,128)(2,1)} %param.18) | copy-start | bytes 12582916
  634.4 337.6 %copy-start.3 = (bf16[1024,2048]{1,0:T(8,128)(2,1)S(1)}, bf16[1024,2048]{1,0:T(8,128)(2,1)}, u32[]{:S(2)}) copy-start(bf16[1024,2048]{1,0:T(8,128)(2,1)} %all-reduce.11.cloned.1.call-done) | copy-start | bytes 12582916
  1011.0 3.2 copy-start.29
  (8 other events, 8.8 us)
Sparse Core Ops, SparseCore 0:
  9.9 30.8 all-gather.11
  42.6 46.6 all-gather.9
  91.2 54.2 all-gather.13
  147.2 55.8 all-gather.15
  270.2 218.1 all-reduce.10
  492.2 53.5 reduce-scatter.8
  549.8 92.0 reduce-scatter.6
  646.1 115.9 reduce-scatter.12
  766.3 116.1 reduce-scatter.10
